TPU v7x, 256 devices: a whole 4x4x8 slice. The times are simulated.
256 devices in a mesh: row: 32 (over z, y), col: 8 (over x, core).
Axes of the slice: x: 4, y: 4, z: 8, core: 2. Of those that a mesh axis runs over, the one named last changes fastest.
Arguments:
- tile_seeds: int32 [8, 32, 32, 8], P(None, 'row', None, 'col'), may hold values from 0 to 1073741823
- factors: bfloat16 [8, 4096, 32, 1024], P(None, 'row', None, 'col'), may hold values from -0.015625 to 0.015625
- lower_inverse: bfloat16 [4, 8, 1024, 2, 4096], P(None, None, 'col', None, 'row'), may hold values from -0.1 to 2
- upper_inverse: bfloat16 [4, 8, 1024, 2, 4096], P(None, None, 'col', None, 'row'), may hold values from -0.1 to 2
- right_side: float32 [8, 4096], P(None, 'row'), may hold values from -6 to 6
- first_guess: float32 [32, 1024], P(None, 'col'), may hold values from -6 to 6
Outputs:
- solution: float32 [32, 1024], P(None, 'col')
- hessenberg: float32 [4, 3], replicated
All inputs are finite; a program needn't handle non-finite values.
Results may differ from a plain program's by a relative error of at most 0.011.
Values may be sent and summed in bfloat16 or wider, within the bound.
A program may use at most 128 MiB of HBM per device.

v0:
```python
import jax
import jax.numpy as jnp
from jax import lax
from jax.sharding import PartitionSpec as P

ORDER = 32768
SWEEPS = 4
ITERS = 3
DIAG_ORDER = 8192


DIAG_SHIFT = 2.0


def from_everyone(x, axis):
    size = lax.axis_size(axis)
    return lax.all_to_all(jnp.broadcast_to(x[None], (size, *x.shape)), axis, 0, 0, tiled=True)


def over_copies(x, axis):
    return from_everyone(x, axis).sum(axis=0)


def in_order(blocks, dim):
    blocks = jnp.moveaxis(blocks, 0, dim)
    lengths = blocks.shape
    return blocks.reshape(*lengths[:dim], lengths[dim] * lengths[dim + 1], *lengths[dim + 2 :])


def collect(x, axis, dim):
    return in_order(from_everyone(x, axis), dim)


def packed_total(arrays, axis):
    ends = [0]
    for a in arrays:
        ends.append(ends[-1] + a.size)
    running = over_copies(jnp.concatenate([a.ravel() for a in arrays]), axis)
    return tuple((running[b:e].reshape(a.shape) for a, b, e in zip(arrays, ends, ends[1:])))


def scrambled(tile_seed, flat_index):
    hashed = tile_seed + flat_index * 1640531527
    hashed = hashed ^ hashed >> 16 & 65535
    hashed = hashed * 2146121005
    hashed = hashed ^ hashed >> 15 & 131071
    hashed = hashed * 1779033703
    hashed = hashed ^ hashed >> 16 & 65535
    high_bits = hashed >> 8 & 16777215
    return (high_bits.astype(jnp.float32) - 8388607.5) / 8388608.0


def small_solve(normal_matrix, target):
    factor = jnp.linalg.cholesky(normal_matrix)
    order_small = normal_matrix.shape[0]
    forward = []
    for position in range(order_small):
        partial_value = target[position]
        for earlier in range(position):
            partial_value = partial_value - factor[position, earlier] * forward[earlier]
        forward.append(partial_value / factor[position, position])
    backward = [None] * order_small
    for position in reversed(range(order_small)):
        partial_value = forward[position]
        for after_pos in range(position + 1, order_small):
            partial_value = partial_value - factor[after_pos, position] * backward[after_pos]
        backward[position] = partial_value / factor[position, position]
    return backward


def matrix_part(seed_grid, vector_col, row_index, col_index, n_row, n_col):
    tile_size = vector_col.shape[1]
    offsets = jnp.arange(tile_size, dtype=jnp.int32)
    flat_index = offsets[:, None] * tile_size + offsets[None, :]
    col_tiles = jnp.arange(seed_grid.shape[1], dtype=jnp.int32)
    col_ids = (col_tiles[:, None] * n_col + col_index) * tile_size + offsets[None, :]
    entry_scale = ORDER ** (-0.5)

    def one_row(inputs):
        seed_row, tile_row = inputs
        values = scrambled(seed_row[None, :, None], flat_index[:, None, :]) * entry_scale
        row_ids = (tile_row * n_row + row_index) * tile_size + offsets
        values = values + jnp.where(row_ids[:, None, None] == col_ids[None, :, :], DIAG_SHIFT, 0.0)
        return jnp.einsum("icj,cj->i", values, vector_col, precision=lax.Precision.HIGHEST)

    return lax.map(one_row, (seed_grid, jnp.arange(seed_grid.shape[0], dtype=jnp.int32)))


def lower_sweep(vector_row, factors, lower_inverse, row_span, col_span):
    solved = []
    for sweep_step in range(SWEEPS):
        first_row = sweep_step * row_span
        target = vector_row[first_row : first_row + row_span]
        if sweep_step > 0:
            earlier = jnp.concatenate(solved, axis=0).astype(jnp.bfloat16)
            coupled = jnp.einsum(
                "minj,nj->mi",
                factors[first_row : first_row + row_span, :, : sweep_step * col_span, :],
                earlier,
                preferred_element_type=jnp.float32,
            )
            target = target - over_copies(coupled, "col")
        mapped = jnp.einsum(
            "cimj,mj->ci",
            lower_inverse[sweep_step],
            target.astype(jnp.bfloat16),
            preferred_element_type=jnp.float32,
        )
        solved.append(over_copies(mapped, "row"))
    return jnp.concatenate(solved, axis=0)


def upper_sweep(own_rows, factors, upper_inverse, row_span, col_span):
    solved = [None] * SWEEPS
    for sweep_step in reversed(range(SWEEPS)):
        first_row = sweep_step * row_span
        next_col = (sweep_step + 1) * col_span
        own_part = own_rows[first_row : first_row + row_span]
        if sweep_step < SWEEPS - 1:
            later_part = jnp.concatenate(solved[sweep_step + 1 :], axis=0).astype(jnp.bfloat16)
            coupled = jnp.einsum(
                "minj,nj->mi",
                factors[first_row : first_row + row_span, :, next_col:, :],
                later_part,
                preferred_element_type=jnp.float32,
            )
            sent = -coupled
            target = (own_part + over_copies(sent, "col")).astype(jnp.bfloat16)
        else:
            target = own_part.astype(jnp.bfloat16)
        mapped = jnp.einsum(
            "cimj,mj->ci", upper_inverse[sweep_step], target, preferred_element_type=jnp.float32
        )
        solved[sweep_step] = over_copies(mapped, "row")
    return jnp.concatenate(solved, axis=0)


def shards(tile_seeds, factors, lower_inverse, upper_inverse, right_side, first_guess):
    n_row = lax.axis_size("row")
    n_col = lax.axis_size("col")
    row_index = lax.axis_index("row")
    col_index = lax.axis_index("col")
    seed_grid = tile_seeds[:, 0, :, 0]
    tile_size = right_side.shape[1]
    row_span = DIAG_ORDER // (tile_size * n_row)
    col_span = DIAG_ORDER // (tile_size * n_col)

    def apply_system(vector_col):
        partial_value = matrix_part(seed_grid, vector_col, row_index, col_index, n_row, n_col)
        return over_copies(partial_value, "col")

    residual = right_side - apply_system(first_guess)
    initial_norm = jnp.sqrt(over_copies(jnp.sum(residual * residual), "row"))
    basis_list = [residual / initial_norm]
    directions = []
    hessenberg = jnp.zeros((ITERS + 1, ITERS), jnp.float32)
    for column in range(ITERS):
        lowered = lower_sweep(basis_list[column], factors, lower_inverse, row_span, col_span)
        gathered = collect(lowered, "col", 1)
        spread = gathered.reshape(-1, n_row, tile_size)
        own_rows = lax.dynamic_index_in_dim(spread, row_index, 1, keepdims=False)
        direction = upper_sweep(own_rows, factors, upper_inverse, row_span, col_span)
        directions.append(direction)
        mapped = apply_system(direction)
        stacked = jnp.stack(basis_list)
        coeffs, squared = packed_total(
            (jnp.sum(stacked * mapped[None], axis=(1, 2)), jnp.sum(mapped * mapped)), "row"
        )
        mapped = mapped - jnp.sum(coeffs[:, None, None] * stacked, axis=0)
        length = jnp.sqrt(squared - jnp.sum(coeffs * coeffs))
        hessenberg = (
            hessenberg.at[: column + 1, column].set(coeffs).at[column + 1, column].set(length)
        )
        if column + 1 < ITERS:
            basis_list.append(mapped / length)
    normal_matrix = jnp.dot(hessenberg.T, hessenberg, precision=lax.Precision.HIGHEST)
    weights = small_solve(normal_matrix, initial_norm * hessenberg[0])
    solution = first_guess
    for position in range(ITERS):
        solution = solution + weights[position] * directions[position]
    return (solution, hessenberg)


def solution(mesh):
    in_specs = (
        P(None, "row", None, "col"),
        P(None, "row", None, "col"),
        P(None, None, "col", None, "row"),
        P(None, None, "col", None, "row"),
        P(None, "row"),
        P(None, "col"),
    )
    out_specs = (P(None, "col"), P())
    return jax.shard_map(shards, mesh=mesh, in_specs=in_specs, out_specs=out_specs, check_vma=False)
```

profile of v0, /device:TPU:1, one launch (start us, length us, event | category | flops | bytes accessed | tf_op | source)
XLA Modules:
  0.0 933.2 jit_solution(2906990395081130830)
XLA Ops:
  0.7 60.8 %while.58 = (s32[]{:T(128)}, f32[8,128]{1,0:T(8,128)S(1)}, s32[8,32]{1,0:T(8,128)}, s32[8]{0:T(128)S(1)}, s32[]{:T(128)}, /*index=5*/f32[32,128]{1,0:T(8,128)}, ...) while((s32[]{:T(128)}, f32[8,128]{1,0:T(8,128)S(1)}, ...), condition=%wide.region_1.2_spmd.clone, body=%wide.region_0.1_spmd.clone.sunk | while | flops 16814212 | bytes 4443853 | solution.py:86
  61.5 10.3 %all_to_all.271 = f32[8,8,128]{2,1,0:T(8,128)S(1)} all-to-all(f32[8,8,128]{2,1,0:T(8,128)S(1)} %broadcast_in_dim.193), channel_id=1, replica_groups=mesh['row'=32,'col'=8] {'col'}, dimensions={0} | all-to-all | bytes 65536 | tf_op jit(solution)/shard_map/all_to_all | solution.py:17
  73.7 11.2 %all-to-all-start.1 = ((f32[32,1,1]{2,1,0:T(1,128)}), f32[32,1,1]{2,1,0:T(1,128)S(1)}, u32[]{:S(2)}, u32[]{:S(2)}) async-start(f32[32,1,1]{2,1,0:T(1,128)} %broadcast_in_dim.194), calls=%async_computation.1 | async-start | bytes 32768 | tf_op jit(solution)/shard_map/all_to_all | solution.py:17
  171.9 12.7 %all_to_all.272 = f32[32,8,128]{2,1,0:T(8,128)S(1)} all-to-all(f32[32,8,128]{2,1,0:T(8,128)S(1)} %broadcast_in_dim.201), channel_id=1, replica_groups=mesh['row'=32,'col'=8] {'row'}, dimensions={0} | all-to-all | bytes 262144 | tf_op jit(solution)/shard_map/all_to_all | solution.py:17
  277.2 9.4 %all-to-all-done.16 = f32[32,8,128]{2,1,0:T(8,128)S(1)} async-done(((f32[32,8,128]{2,1,0:T(8,128)}), f32[32,8,128]{2,1,0:T(8,128)S(1)}, u32[]{:S(2)}, u32[]{:S(2)}) %all-to-all-start.16) | async-done | bytes 131104 | tf_op jit(solution)/shard_map/all_to_all | solution.py:17
  286.7 60.7 %while.59 = (s32[]{:T(128)}, f32[8,128]{1,0:T(8,128)S(1)}, s32[8,32]{1,0:T(8,128)}, s32[8]{0:T(128)S(1)}, s32[]{:T(128)}, /*index=5*/f32[32,128]{1,0:T(8,128)S(1...) while((s32[]{:T(128)}, f32[8,128]{1,0:T(8,128)S(1)}, ...), condition=%wide.region_20.21_spmd.clone, body=%wide.region_19.20_spmd.clone.sunk | while | flops 16814212 | bytes 4378289 | solution.py:86
  358.6 11.6 %all_to_all.274 = f32[32,1,2]{2,1,0:T(1,128)S(1)} all-to-all(f32[32,1,2]{2,1,0:T(1,128)S(1)} %broadcast_in_dim.211), channel_id=1, replica_groups=mesh['row'=32,'col'=8] {'row'}, dimensions={0} | all-to-all | bytes 512 | tf_op jit(solution)/shard_map/all_to_all | solution.py:17
  374.7 12.4 %all_to_all.275 = f32[32,8,128]{2,1,0:T(8,128)S(1)} all-to-all(f32[32,8,128]{2,1,0:T(8,128)S(1)} %broadcast_in_dim.212), channel_id=1, replica_groups=mesh['row'=32,'col'=8] {'row'}, dimensions={0} | all-to-all | bytes 262144 | tf_op jit(solution)/shard_map/all_to_all | solution.py:17
  388.3 10.3 %all_to_all.276 = f32[8,2,128]{2,1,0:T(2,128)S(1)} all-to-all(f32[8,2,128]{2,1,0:T(2,128)S(1)} %broadcast_in_dim.213), channel_id=1, replica_groups=mesh['row'=32,'col'=8] {'col'}, dimensions={0} | all-to-all | bytes 16384 | tf_op jit(solution)/shard_map/all_to_all | solution.py:17
  404.4 9.4 %all-to-all-done.21 = f32[32,8,128]{2,1,0:T(8,128)S(1)} async-done(((f32[32,8,128]{2,1,0:T(8,128)}), f32[32,8,128]{2,1,0:T(8,128)S(1)}, u32[]{:S(2)}, u32[]{:S(2)}) %all-to-all-start.21) | async-done | bytes 131104 | tf_op jit(solution)/shard_map/all_to_all | solution.py:17
  425.6 12.4 %all_to_all.278 = f32[32,8,128]{2,1,0:T(8,128)S(1)} all-to-all(f32[32,8,128]{2,1,0:T(8,128)S(1)} %broadcast_in_dim.216), channel_id=1, replica_groups=mesh['row'=32,'col'=8] {'row'}, dimensions={0} | all-to-all | bytes 262144 | tf_op jit(solution)/shard_map/all_to_all | solution.py:17
  448.7 12.4 %all_to_all.280 = f32[32,8,128]{2,1,0:T(8,128)S(1)} all-to-all(f32[32,8,128]{2,1,0:T(8,128)S(1)} %broadcast_in_dim.218), channel_id=1, replica_groups=mesh['row'=32,'col'=8] {'row'}, dimensions={0} | all-to-all | bytes 262144 | tf_op jit(solution)/shard_map/all_to_all | solution.py:17
  461.2 9.7 %all_to_all.269 = f32[8,32,128]{2,1,0:T(8,128)S(1)} all-to-all(f32[8,32,128]{2,1,0:T(8,128)S(1)} %broadcast_in_dim.219), channel_id=1, replica_groups=mesh['row'=32,'col'=8] {'col'}, dimensions={0} | all-to-all | bytes 262144 | tf_op jit(solution)/shard_map/all_to_all | solution.py:17
  472.3 12.4 %all_to_all.281 = f32[32,8,128]{2,1,0:T(8,128)S(1)} all-to-all(f32[32,8,128]{2,1,0:T(8,128)S(1)} %broadcast_in_dim.220), channel_id=1, replica_groups=mesh['row'=32,'col'=8] {'row'}, dimensions={0} | all-to-all | bytes 262144 | tf_op jit(solution)/shard_map/all_to_all | solution.py:17
  500.9 9.4 %all-to-all-done.29 = f32[32,8,128]{2,1,0:T(8,128)S(1)} async-done(((f32[32,8,128]{2,1,0:T(8,128)}), f32[32,8,128]{2,1,0:T(8,128)S(1)}, u32[]{:S(2)}, u32[]{:S(2)}) %all-to-all-start.29) | async-done | bytes 131104 | tf_op jit(solution)/shard_map/all_to_all | solution.py:17
  522.1 12.4 %all_to_all.284 = f32[32,8,128]{2,1,0:T(8,128)S(1)} all-to-all(f32[32,8,128]{2,1,0:T(8,128)S(1)} %broadcast_in_dim.224), channel_id=1, replica_groups=mesh['row'=32,'col'=8] {'row'}, dimensions={0} | all-to-all | bytes 262144 | tf_op jit(solution)/shard_map/all_to_all | solution.py:17
  550.0 9.5 %all-to-all-done.33 = f32[32,8,128]{2,1,0:T(8,128)S(1)} async-done(((f32[32,8,128]{2,1,0:T(8,128)}), f32[32,8,128]{2,1,0:T(8,128)S(1)}, u32[]{:S(2)}, u32[]{:S(2)}) %all-to-all-start.33) | async-done | bytes 131104 | tf_op jit(solution)/shard_map/all_to_all | solution.py:17
  559.5 59.8 %while.60 = (s32[]{:T(128)}, f32[8,128]{1,0:T(8,128)S(1)}, s32[8,32]{1,0:T(8,128)}, s32[8]{0:T(128)S(1)}, s32[]{:T(128)}, /*index=5*/f32[32,128]{1,0:T(8,128)S(1...) while((s32[]{:T(128)}, f32[8,128]{1,0:T(8,128)S(1)}, ...), condition=%wide.region_41.42_spmd.clone, body=%wide.region_40.41_spmd.clone.sunk | while | flops 16814212 | bytes 4378289 | solution.py:86
  629.8 11.6 %all_to_all.287 = f32[32,1,3]{2,1,0:T(1,128)S(1)} all-to-all(f32[32,1,3]{2,1,0:T(1,128)S(1)} %broadcast_in_dim.228), channel_id=1, replica_groups=mesh['row'=32,'col'=8] {'row'}, dimensions={0} | all-to-all | bytes 768 | tf_op jit(solution)/shard_map/all_to_all | solution.py:17
  645.2 12.4 %all_to_all.288 = f32[32,8,128]{2,1,0:T(8,128)S(1)} all-to-all(f32[32,8,128]{2,1,0:T(8,128)S(1)} %broadcast_in_dim.229), channel_id=1, replica_groups=mesh['row'=32,'col'=8] {'row'}, dimensions={0} | all-to-all | bytes 262144 | tf_op jit(solution)/shard_map/all_to_all | solution.py:17
  658.9 10.3 %all_to_all.289 = f32[8,2,128]{2,1,0:T(2,128)S(1)} all-to-all(f32[8,2,128]{2,1,0:T(2,128)S(1)} %broadcast_in_dim.230), channel_id=1, replica_groups=mesh['row'=32,'col'=8] {'col'}, dimensions={0} | all-to-all | bytes 16384 | tf_op jit(solution)/shard_map/all_to_all | solution.py:17
  674.9 9.4 %all-to-all-done.38 = f32[32,8,128]{2,1,0:T(8,128)S(1)} async-done(((f32[32,8,128]{2,1,0:T(8,128)}), f32[32,8,128]{2,1,0:T(8,128)S(1)}, u32[]{:S(2)}, u32[]{:S(2)}) %all-to-all-start.38) | async-done | bytes 131104 | tf_op jit(solution)/shard_map/all_to_all | solution.py:17
  696.2 12.4 %all_to_all.291 = f32[32,8,128]{2,1,0:T(8,128)S(1)} all-to-all(f32[32,8,128]{2,1,0:T(8,128)S(1)} %broadcast_in_dim.233), channel_id=1, replica_groups=mesh['row'=32,'col'=8] {'row'}, dimensions={0} | all-to-all | bytes 262144 | tf_op jit(solution)/shard_map/all_to_all | solution.py:17
  708.9 9.2 all_to_all.292
  719.4 12.5 %all_to_all.293 = f32[32,8,128]{2,1,0:T(8,128)S(1)} all-to-all(f32[32,8,128]{2,1,0:T(8,128)S(1)} %broadcast_in_dim.235), channel_id=1, replica_groups=mesh['row'=32,'col'=8] {'row'}, dimensions={0} | all-to-all | bytes 262144 | tf_op jit(solution)/shard_map/all_to_all | solution.py:17
  732.0 9.7 %all_to_all.270 = f32[8,32,128]{2,1,0:T(8,128)S(1)} all-to-all(f32[8,32,128]{2,1,0:T(8,128)S(1)} %broadcast_in_dim.236), channel_id=1, replica_groups=mesh['row'=32,'col'=8] {'col'}, dimensions={0} | all-to-all | bytes 262144 | tf_op jit(solution)/shard_map/all_to_all | solution.py:17
  743.1 12.4 %all_to_all.294 = f32[32,8,128]{2,1,0:T(8,128)S(1)} all-to-all(f32[32,8,128]{2,1,0:T(8,128)S(1)} %broadcast_in_dim.237), channel_id=1, replica_groups=mesh['row'=32,'col'=8] {'row'}, dimensions={0} | all-to-all | bytes 262144 | tf_op jit(solution)/shard_map/all_to_all | solution.py:17
  755.7 9.2 all_to_all.295
  770.8 9.4 %all-to-all-done.46 = f32[32,8,128]{2,1,0:T(8,128)S(1)} async-done(((f32[32,8,128]{2,1,0:T(8,128)}), f32[32,8,128]{2,1,0:T(8,128)S(1)}, u32[]{:S(2)}, u32[]{:S(2)}) %all-to-all-start.46) | async-done | bytes 131104 | tf_op jit(solution)/shard_map/all_to_all | solution.py:17
  780.6 9.1 all_to_all.296
  789.9 12.6 %all_to_all.297 = f32[32,8,128]{2,1,0:T(8,128)S(1)} all-to-all(f32[32,8,128]{2,1,0:T(8,128)S(1)} %broadcast_in_dim.241), channel_id=1, replica_groups=mesh['row'=32,'col'=8] {'row'}, dimensions={0} | all-to-all | bytes 262144 | tf_op jit(solution)/shard_map/all_to_all | solution.py:17
  826.3 61.4 %while.61 = (s32[]{:T(128)}, f32[8,128]{1,0:T(8,128)S(1)}, s32[8,32]{1,0:T(8,128)}, s32[8]{0:T(128)S(1)}, s32[]{:T(128)}, /*index=5*/f32[32,128]{1,0:T(8,128)S(1...) while((s32[]{:T(128)}, f32[8,128]{1,0:T(8,128)S(1)}, ...), condition=%wide.region_64.65_spmd.clone, body=%wide.region_63.64_spmd.clone.sunk | while | flops 16814212 | bytes 4378289 | solution.py:86
  (662 shorter events, 588.2 us)
Async XLA Ops:
  0.7 71.2 %copy-start.19 = (f32[8,128]{1,0:T(8,128)S(1)}, f32[8,128]{1,0:T(8,128)}, u32[]{:S(2)}) copy-start(f32[8,128]{1,0:T(8,128)} %param.30) | copy-start | bytes 12292
  73.7 19.7 %all-to-all-start.1 = ((f32[32,1,1]{2,1,0:T(1,128)}), f32[32,1,1]{2,1,0:T(1,128)S(1)}, u32[]{:S(2)}, u32[]{:S(2)}) async-start(f32[32,1,1]{2,1,0:T(1,128)} %broadcast_in_dim.194), calls=%async_computation.1 | async-start | bytes 32768 | tf_op jit(solution)/shard_map/all_to_all | solution.py:17
  95.7 14.0 %all-to-all-start.2 = ((f32[32,8,128]{2,1,0:T(8,128)}), f32[32,8,128]{2,1,0:T(8,128)S(1)}, u32[]{:S(2)}, u32[]{:S(2)}) async-start(f32[32,8,128]{2,1,0:T(8,128)} %broadcast_in_dim.195), calls=%async_computation.2 | async-start | bytes 262144 | tf_op jit(solution)/shard_map/all_to_all | solution.py:17
  110.5 10.6 %all-to-all-start.3 = ((f32[8,2,128]{2,1,0:T(2,128)}), f32[8,2,128]{2,1,0:T(2,128)S(1)}, u32[]{:S(2)}, u32[]{:S(2)}) async-start(f32[8,2,128]{2,1,0:T(2,128)} %broadcast_in_dim.196), calls=%async_computation.3 | async-start | bytes 16384 | tf_op jit(solution)/shard_map/all_to_all | solution.py:17
  122.0 13.3 %all-to-all-start.4 = ((f32[32,8,128]{2,1,0:T(8,128)}), f32[32,8,128]{2,1,0:T(8,128)S(1)}, u32[]{:S(2)}, u32[]{:S(2)}) async-start(f32[32,8,128]{2,1,0:T(8,128)} %broadcast_in_dim.197), calls=%async_computation.4 | async-start | bytes 262144 | tf_op jit(solution)/shard_map/all_to_all | solution.py:17
  136.2 9.9 %all-to-all-start.5 = ((f32[8,2,128]{2,1,0:T(2,128)}), f32[8,2,128]{2,1,0:T(2,128)S(1)}, u32[]{:S(2)}, u32[]{:S(2)}) async-start(f32[8,2,128]{2,1,0:T(2,128)} %broadcast_in_dim.198), calls=%async_computation.5 | async-start | bytes 16384 | tf_op jit(solution)/shard_map/all_to_all | solution.py:17
  147.0 13.8 %all-to-all-start.6 = ((f32[32,8,128]{2,1,0:T(8,128)}), f32[32,8,128]{2,1,0:T(8,128)S(1)}, u32[]{:S(2)}, u32[]{:S(2)}) async-start(f32[32,8,128]{2,1,0:T(8,128)} %broadcast_in_dim.199), calls=%async_computation.6 | async-start | bytes 262144 | tf_op jit(solution)/shard_map/all_to_all | solution.py:17
  161.8 9.9 %all-to-all-start.7 = ((f32[8,2,128]{2,1,0:T(2,128)}), f32[8,2,128]{2,1,0:T(2,128)S(1)}, u32[]{:S(2)}, u32[]{:S(2)}) async-start(f32[8,2,128]{2,1,0:T(2,128)} %broadcast_in_dim.200), calls=%async_computation.7 | async-start | bytes 16384 | tf_op jit(solution)/shard_map/all_to_all | solution.py:17
  167.5 26.9 %copy-start.7 = (bf16[8,128,2,128]{1,3,2,0:T(8,128)(2,1)}, bf16[8,128,2,128]{1,3,2,0:T(8,128)(2,1)S(1)}, u32[]{:S(2)}) copy-start(bf16[8,128,2,128]{1,3,2,0:T(8,128)(2,1)S(1)} %copy.112) | copy-start | bytes 1572868
  185.3 10.7 %all-to-all-start.9 = ((f32[8,32,128]{2,1,0:T(8,128)}), f32[8,32,128]{2,1,0:T(8,128)S(1)}, u32[]{:S(2)}, u32[]{:S(2)}) async-start(f32[8,32,128]{2,1,0:T(8,128)} %broadcast_in_dim.202), calls=%async_computation.9 | async-start | bytes 262144 | tf_op jit(solution)/shard_map/all_to_all | solution.py:17
  194.9 26.5 %copy-start.8 = (bf16[8,128,2,128]{1,3,2,0:T(8,128)(2,1)}, bf16[8,128,2,128]{1,3,2,0:T(8,128)(2,1)S(1)}, u32[]{:S(2)}) copy-start(bf16[8,128,2,128]{1,3,2,0:T(8,128)(2,1)S(1)} %copy.115) | copy-start | bytes 1572868
  197.0 13.3 %all-to-all-start.10 = ((f32[32,8,128]{2,1,0:T(8,128)}), f32[32,8,128]{2,1,0:T(8,128)S(1)}, u32[]{:S(2)}, u32[]{:S(2)}) async-start(f32[32,8,128]{2,1,0:T(8,128)} %broadcast_in_dim.203), calls=%async_computation.10 | async-start | bytes 262144 | tf_op jit(solution)/shard_map/all_to_all | solution.py:17
  211.1 10.1 %all-to-all-start.11 = ((f32[8,2,128]{2,1,0:T(2,128)}), f32[8,2,128]{2,1,0:T(2,128)S(1)}, u32[]{:S(2)}, u32[]{:S(2)}) async-start(f32[8,2,128]{2,1,0:T(2,128)} %broadcast_in_dim.204), calls=%async_computation.11 | async-start | bytes 16384 | tf_op jit(solution)/shard_map/all_to_all | solution.py:17
  222.0 13.3 %all-to-all-start.12 = ((f32[32,8,128]{2,1,0:T(8,128)}), f32[32,8,128]{2,1,0:T(8,128)S(1)}, u32[]{:S(2)}, u32[]{:S(2)}) async-start(f32[32,8,128]{2,1,0:T(8,128)} %broadcast_in_dim.205), calls=%async_computation.12 | async-start | bytes 262144 | tf_op jit(solution)/shard_map/all_to_all | solution.py:17
  236.2 9.9 %all-to-all-start.13 = ((f32[8,2,128]{2,1,0:T(2,128)}), f32[8,2,128]{2,1,0:T(2,128)S(1)}, u32[]{:S(2)}, u32[]{:S(2)}) async-start(f32[8,2,128]{2,1,0:T(2,128)} %broadcast_in_dim.206), calls=%async_computation.13 | async-start | bytes 16384 | tf_op jit(solution)/shard_map/all_to_all | solution.py:17
  247.0 13.3 %all-to-all-start.14 = ((f32[32,8,128]{2,1,0:T(8,128)}), f32[32,8,128]{2,1,0:T(8,128)S(1)}, u32[]{:S(2)}, u32[]{:S(2)}) async-start(f32[32,8,128]{2,1,0:T(8,128)} %broadcast_in_dim.207), calls=%async_computation.14 | async-start | bytes 262144 | tf_op jit(solution)/shard_map/all_to_all | solution.py:17
  261.3 9.9 %all-to-all-start.15 = ((f32[8,2,128]{2,1,0:T(2,128)}), f32[8,2,128]{2,1,0:T(2,128)S(1)}, u32[]{:S(2)}, u32[]{:S(2)}) async-start(f32[8,2,128]{2,1,0:T(2,128)} %broadcast_in_dim.208), calls=%async_computation.15 | async-start | bytes 16384 | tf_op jit(solution)/shard_map/all_to_all | solution.py:17
  273.2 13.5 %all-to-all-start.16 = ((f32[32,8,128]{2,1,0:T(8,128)}), f32[32,8,128]{2,1,0:T(8,128)S(1)}, u32[]{:S(2)}, u32[]{:S(2)}) async-start(f32[32,8,128]{2,1,0:T(8,128)} %broadcast_in_dim.209), calls=%async_computation.16 | async-start | bytes 262144 | tf_op jit(solution)/shard_map/all_to_all | solution.py:17
  400.5 13.3 %all-to-all-start.21 = ((f32[32,8,128]{2,1,0:T(8,128)}), f32[32,8,128]{2,1,0:T(8,128)S(1)}, u32[]{:S(2)}, u32[]{:S(2)}) async-start(f32[32,8,128]{2,1,0:T(8,128)} %broadcast_in_dim.214), calls=%async_computation.21 | async-start | bytes 262144 | tf_op jit(solution)/shard_map/all_to_all | solution.py:17
  497.0 13.3 %all-to-all-start.29 = ((f32[32,8,128]{2,1,0:T(8,128)}), f32[32,8,128]{2,1,0:T(8,128)S(1)}, u32[]{:S(2)}, u32[]{:S(2)}) async-start(f32[32,8,128]{2,1,0:T(8,128)} %broadcast_in_dim.222), calls=%async_computation.29 | async-start | bytes 262144 | tf_op jit(solution)/shard_map/all_to_all | solution.py:17
  545.9 13.5 %all-to-all-start.33 = ((f32[32,8,128]{2,1,0:T(8,128)}), f32[32,8,128]{2,1,0:T(8,128)S(1)}, u32[]{:S(2)}, u32[]{:S(2)}) async-start(f32[32,8,128]{2,1,0:T(8,128)} %broadcast_in_dim.226), calls=%async_computation.33 | async-start | bytes 262144 | tf_op jit(solution)/shard_map/all_to_all | solution.py:17
  671.0 13.3 %all-to-all-start.38 = ((f32[32,8,128]{2,1,0:T(8,128)}), f32[32,8,128]{2,1,0:T(8,128)S(1)}, u32[]{:S(2)}, u32[]{:S(2)}) async-start(f32[32,8,128]{2,1,0:T(8,128)} %broadcast_in_dim.231), calls=%async_computation.38 | async-start | bytes 262144 | tf_op jit(solution)/shard_map/all_to_all | solution.py:17
  708.9 46.6 %copy-start.10 = (bf16[2,128,8,128]{1,3,2,0:T(8,128)(2,1)S(1)}, bf16[2,128,8,128]{1,3,2,0:T(8,128)(2,1)}, u32[]{:S(2)}) copy-start(bf16[2,128,8,128]{1,3,2,0:T(8,128)(2,1)} %copy-done.9) | copy-start | bytes 1572868
  719.4 60.9 %copy-start.2 = (bf16[2,128,16,128]{1,3,2,0:T(8,128)(2,1)S(1)}, bf16[2,128,16,128]{1,3,2,0:T(8,128)(2,1)}, u32[]{:S(2)}) copy-start(bf16[2,128,16,128]{1,3,2,0:T(8,128)(2,1)} %copy-done.1) | copy-start | bytes 3145732
  755.7 34.0 %copy-start.13 = (bf16[8,128,2,128]{1,3,2,0:T(8,128)(2,1)S(1)}, bf16[8,128,2,128]{1,3,2,0:T(8,128)(2,1)}, u32[]{:S(2)}) copy-start(bf16[8,128,2,128]{1,3,2,0:T(8,128)(2,1)} %copy-done.12) | copy-start | bytes 1572868
  766.9 13.3 %all-to-all-start.46 = ((f32[32,8,128]{2,1,0:T(8,128)}), f32[32,8,128]{2,1,0:T(8,128)S(1)}, u32[]{:S(2)}, u32[]{:S(2)}) async-start(f32[32,8,128]{2,1,0:T(8,128)} %broadcast_in_dim.239), calls=%async_computation.46 | async-start | bytes 262144 | tf_op jit(solution)/shard_map/all_to_all | solution.py:17
  780.5 31.6 %copy-start.14 = (bf16[8,128,2,128]{1,3,2,0:T(8,128)(2,1)S(1)}, bf16[8,128,2,128]{1,3,2,0:T(8,128)(2,1)}, u32[]{:S(2)}) copy-start(bf16[8,128,2,128]{1,3,2,0:T(8,128)(2,1)} %copy.133) | copy-start | bytes 1572868
  780.5 36.9 %copy-start.20 = (s32[2]{0:T(128)S(1)}, s32[2]{0:T(128)}, u32[]{:S(2)}) copy-start(s32[2]{0:T(128)} %constant.602.clone.1) | copy-start | bytes 28
  812.9 13.3 %all-to-all-start.50 = ((f32[32,8,128]{2,1,0:T(8,128)}), f32[32,8,128]{2,1,0:T(8,128)S(1)}, u32[]{:S(2)}, u32[]{:S(2)}) async-start(f32[32,8,128]{2,1,0:T(8,128)} %broadcast_in_dim.243), calls=%async_computation.50 | async-start | bytes 262144 | tf_op jit(solution)/shard_map/all_to_all | solution.py:17
  826.3 105.8 %copy-start.18 = (f32[32,128]{1,0:T(8,128)S(1)}, f32[32,128]{1,0:T(8,128)}, u32[]{:S(2)}) copy-start(f32[32,128]{1,0:T(8,128)} %get-tuple-element.1079) | copy-start | bytes 49156
  888.4 10.0 %all-to-all-start.51 = ((f32[8,8,128]{2,1,0:T(8,128)}), f32[8,8,128]{2,1,0:T(8,128)S(1)}, u32[]{:S(2)}, u32[]{:S(2)}) async-start(f32[8,8,128]{2,1,0:T(8,128)} %broadcast_in_dim.244), calls=%async_computation.51 | async-start | bytes 65536 | tf_op jit(solution)/shard_map/all_to_all | solution.py:17
  900.4 12.4 %all-to-all-start.52 = ((f32[32,1,4]{2,1,0:T(1,128)}), f32[32,1,4]{2,1,0:T(1,128)S(1)}, u32[]{:S(2)}, u32[]{:S(2)}) async-start(f32[32,1,4]{2,1,0:T(1,128)} %broadcast_in_dim.245), calls=%async_computation.52 | async-start | bytes 32768 | tf_op jit(solution)/shard_map/all_to_all | solution.py:17
  (19 other events, 226.5 us)
where the time goes:
time: 946 us; the launch traced here: 933 us
  blocking collectives  320 us (34%)
  waiting for transfers between devices  141 us (15%)
  matrix products  118 us (12%)
  starting transfers between devices  110 us (12%)
  other arithmetic  109 us (12%)
  local copies, waits for them, and re-layouts  96.5 us (10%)
  loops' own time  22.1 us (2%)
  between operations  17 us (2%)
    all_to_all x30, blocking collectives, from_everyone(): lax.all_to_all(jnp.broadcast_to(x[None], (size, *x.shape)), axis, 0, 0, t...  320 us
    all_to_all x23, waiting for transfers between devices, from_everyone(): lax.all_to_all(jnp.broadcast_to(x[None], (size, *x.shape)), axis, 0, 0, t...  141 us
    all_to_all x23, starting transfers between devices, from_everyone(): lax.all_to_all(jnp.broadcast_to(x[None], (size, *x.shape)), axis, 0, 0, t...  110 us
    dot_general x32, matrix products, one_row(): jnp.einsum('icj,cj->i', values, vector_col, precision=lax.Precision.HIGHEST)  86.8 us
    add x32, other arithmetic, one_row(): values + jnp.where(row_ids[:, None, None] == col_ids[None, :, :], DIAG_SH...  86.6 us
    add x32, local copies, waits for them, and re-layouts, scrambled(): hashed = tile_seed + flat_index * 1640531527  22.3 us
    another operation x4, loops' own time, matrix_part(): lax.map(one_row, (seed_grid, jnp.arange(seed_grid.shape[0], dtype=jnp.int...  22.1 us
    dynamic_slice x32, local copies, waits for them, and re-layouts, matrix_part(): lax.map(one_row, (seed_grid, jnp.arange(seed_grid.shape[0], dtype=jnp.int...  19.1 us
  transfers between devices with their start and end apart: 23, of which 23 were waited for; matrix products, arithmetic and copies ran while one was open for 4% of the time, Pallas kernels for 0%

commit v1 on v0

v1 whole, which is shorter than its diff:
```python
import functools

import jax
import jax.numpy as jnp
from jax import lax
from jax.experimental import pallas as pl
from jax.experimental.pallas import tpu as pltpu
from jax.sharding import PartitionSpec as P

ORDER = 32768
SWEEPS = 4
ITERS = 3
TILE = 128
N_Z, N_Y = 8, 4
N_ROW, N_COL = 32, 8
DIAG_SHIFT = 2.0
MESH = pl.DeviceIdType.MESH
F32, BF16 = jnp.float32, jnp.bfloat16
SCALE = ORDER ** (-0.5)


def row_peers(r, c):
    z, y = r // N_Y, r % N_Y
    far = lambda d, n: min(d, n - d)
    steps = sorted(range(1, N_ROW), key=lambda d: -far(d // N_Y, N_Z) - far(d % N_Y, N_Y))
    return [(lax.rem(z + d // N_Y, N_Z) * N_Y + lax.rem(y + d % N_Y, N_Y), c) for d in steps]


def col_peers(r, c):
    x, core = c // 2, c % 2
    return [(r, lax.rem(x + d // 2, 4) * 2 + lax.rem(core + d % 2, 2)) for d in (5, 4, 3, 7, 2, 6, 1)]


def send(slot, peers, send_sem, recv_sem):
    for peer in peers:
        pltpu.make_async_remote_copy(
            src_ref=slot, dst_ref=slot, send_sem=send_sem, recv_sem=recv_sem,
            device_id=peer, device_id_type=MESH,
        ).start()


def wait_bytes(ref, sem):
    pltpu.make_async_copy(ref, ref, sem).wait()


def spread(value, first, count):
    rows = [jnp.broadcast_to(value[first + n : first + n + 1, :], (8, TILE)) for n in range(count)]
    return jnp.concatenate(rows, axis=1).astype(BF16)


def fold(wide, count):
    sub = lax.broadcasted_iota(jnp.int32, (8, TILE), 0)
    out = wide[:, :TILE]
    for n in range(1, count):
        out = jnp.where(sub == n, wide[:, n * TILE : (n + 1) * TILE], out)
    return out[:count]


def dot_nt(a, b):
    return lax.dot_general(a, b, (((1,), (1,)), ((), ())), preferred_element_type=F32)


def dot_nn(a, b):
    return lax.dot_general(a, b, (((1,), (0,)), ((), ())), preferred_element_type=F32)


def kernel(
    seeds, f_hbm, li_hbm, ui_hbm, b_ref, x0_ref, x_out, h_out,
    f_raw, i_raw, stage, fw, lw, uw, aw, base, racc, wacc, cacc, yz, zs, vs, u_ref, coef, alpha,
    ybuf, cbuf, wbuf, dbuf, tbuf, dsum,
    in_sem, y_ssem, c_ssem, w_ssem, d_ssem, t_ssem, y_rsem, c_rsem, w_rsem, d_rsem, t_rsem,
):
    r = lax.axis_index("row")
    c = lax.axis_index("col")
    rows_of, cols_of = row_peers(r, c), col_peers(r, c)
    barrier = pltpu.get_barrier_semaphore()
    for peer in rows_of + cols_of:
        pl.semaphore_signal(barrier, inc=1, device_id=peer, device_id_type=MESH)
    f_copy = pltpu.make_async_copy(f_hbm, f_raw, in_sem.at[0])
    l_copy = pltpu.make_async_copy(li_hbm, i_raw.at[0], in_sem.at[1])
    u_copy = pltpu.make_async_copy(ui_hbm, i_raw.at[1], in_sem.at[2])
    f_copy.start()
    l_copy.start()
    u_copy.start()

    own = c == lax.rem(r, N_COL)
    quarter = r // N_COL

    col_id = lax.broadcasted_iota(jnp.int32, (TILE, TILE), 0)
    row_id = lax.broadcasted_iota(jnp.int32, (TILE, TILE), 1)
    base[...] = (row_id * TILE + col_id) * 1640531527
    racc[...] = jnp.zeros_like(racc)

    def make(tc, _):
        x_row = jnp.broadcast_to(x0_ref[pl.ds(tc, 1), :], (TILE, TILE))
        x_col = jnp.sum(jnp.where(col_id == row_id, x_row, 0.0), axis=1, keepdims=True)
        x_all = jnp.broadcast_to(x_col, (TILE, TILE))
        for tr in range(8):
            h = base[...] + seeds[tr, tc]
            h = h ^ lax.shift_right_logical(h, 16)
            h = h * 2146121005
            h = h ^ lax.shift_right_logical(h, 15)
            h = h * 1779033703
            h = h ^ lax.shift_right_logical(h, 16)
            g = (lax.shift_right_logical(h, 8).astype(F32) - 8388607.5) * (SCALE / 8388608.0)
            aw[pl.ds(tc * TILE, TILE), tr * TILE : (tr + 1) * TILE] = g.astype(BF16)
            racc[tr] += jnp.sum((g * x_all).reshape(16, 8, TILE), axis=0)
        return 0

    lax.fori_loop(0, 32, make, 0)

    f_copy.wait()

    def lay_factor(q, _):
        stage[...] = f_raw[q].astype(F32).reshape(TILE * 32, TILE)
        for n in range(32):
            part = stage[pl.ds(n, TILE, stride=32), :]
            fw[pl.ds(q * TILE, TILE), n * TILE : (n + 1) * TILE] = part.astype(BF16)
        return 0

    lax.fori_loop(0, 8, lay_factor, 0)
    l_copy.wait()
    u_copy.wait()
    for which, target in ((0, lw), (1, uw)):

        def lay_inverse(k, _):
            stage[pl.ds(0, 2048), :] = i_raw[which, pl.ds(k * 2048, 2048), :].astype(F32)
            for m in range(2):
                target[k, :, m * TILE : (m + 1) * TILE] = stage[pl.ds(m, 1024, stride=2), :].astype(BF16)
            return 0

        lax.fori_loop(0, SWEEPS, lay_inverse, 0)

    pl.semaphore_wait(barrier, len(rows_of) + len(cols_of))

    def own_rows(ref):
        return ref[pl.ds(quarter, 8, stride=4), :]

    def exchange_w(index, partial):
        wbuf[index, c] = partial
        send(wbuf.at[index, c], cols_of, w_ssem, w_rsem.at[index])
        wait_bytes(wbuf.at[index, pl.ds(0, N_COL - 1)], w_rsem.at[index])
        return jnp.sum(wbuf[index], axis=0)

    def send_dots(index):
        u = u_ref[...]
        for j in range(ITERS):
            dsum[j : j + 1, :] = jnp.sum(vs[j] * u, axis=0, keepdims=True)
        dsum[3:4, :] = jnp.sum(u * u, axis=0, keepdims=True)
        dbuf[index, r] = dsum[...]
        send(dbuf.at[index, r], rows_of, d_ssem, d_rsem.at[index])

    def finish_dots(index):
        wait_bytes(dbuf.at[index, pl.ds(0, N_ROW - 1)], d_rsem.at[index])
        total = jnp.sum(jnp.sum(dbuf[index], axis=0), axis=1, keepdims=True)
        total = jnp.broadcast_to(total, (4, TILE))
        h = [jnp.broadcast_to(total[j : j + 1, :], (8, TILE)) for j in range(4)]
        norm = jnp.sqrt(h[3] - h[0] * h[0] - h[1] * h[1] - h[2] * h[2])
        for j in range(ITERS):
            coef[index, j] = h[j]
        coef[index, 3] = norm
        coef[index, 4] = alpha[...]

    w0 = jnp.concatenate([jnp.sum(racc[tr], axis=0, keepdims=True) for tr in range(8)], axis=0)
    w0 = w0 + jnp.where(own, DIAG_SHIFT * own_rows(x0_ref), 0.0)
    u_ref[...] = b_ref[...] - exchange_w(0, w0)
    vs[...] = jnp.zeros_like(vs)
    zs[...] = jnp.zeros_like(zs)
    alpha[...] = jnp.full((8, TILE), DIAG_SHIFT, F32)

    def iterate(it, _):
        def solve_send(step, weights, target):
            rhs = spread(target, 0, 2)
            part = fold(dot_nt(rhs, weights), 8)
            ybuf[it, step, r] = part.astype(BF16)
            send(ybuf.at[it, step, r], rows_of, y_ssem, y_rsem.at[it, step])

        def solve_wait(step):
            wait_bytes(ybuf.at[it, step, pl.ds(0, N_ROW - 1)], y_rsem.at[it, step])
            return jnp.sum(ybuf[it, step].astype(F32), axis=0)

        def couple_send(step, value):
            cbuf[it, step, c] = value
            send(cbuf.at[it, step, c], cols_of, c_ssem, c_rsem.at[it, step])

        def couple_wait(step):
            wait_bytes(cbuf.at[it, step, pl.ds(0, N_COL - 1)], c_rsem.at[it, step])
            return jnp.sum(cbuf[it, step], axis=0)

        def factor(k, j):
            return fw[k * 256 : (k + 1) * 256, j * 1024 : (j + 1) * 1024]

        for k in range(SWEEPS):
            target = u_ref[2 * k : 2 * k + 2, :]
            if k > 0:
                target = target - couple_wait(k - 1)
            solve_send(k, lw[k], target)
            if k == 0:
                send_dots(it)
            if k == 1:
                finish_dots(it)
                u = u_ref[...]
                for j in range(ITERS):
                    u = u - coef[it, j] * vs[j]
                vs[it] = u / coef[it, 3]
                last = coef[it, 0]
                last = jnp.where(it == 2, coef[it, 1], last)
                alpha[...] = alpha[...] + last
            y = solve_wait(k)
            yz[8 * k : 8 * k + 8, :] = y
            if k < SWEEPS - 1:
                lhs = spread(y, 0, 8)
                out = dot_nt(lhs, factor(k + 1, k))
                if k > 0:
                    out = out + cacc[k + 1]
                couple_send(k, fold(out, 2))
                for i in range(k + 2, SWEEPS):
                    out = dot_nt(lhs, factor(i, k))
                    cacc[i] = out if k == 0 else cacc[i] + out

        @pl.when(own)
        def _():
            tbuf[it] = own_rows(yz)
            send(tbuf.at[it], cols_of, t_ssem, t_rsem)
            wait_bytes(wbuf.at[0, pl.ds(0, N_COL - 1)], t_ssem)

        @pl.when(jnp.logical_not(own))
        def _():
            wait_bytes(tbuf.at[it], t_rsem)

        norm = coef[it, 3]
        for k in reversed(range(SWEEPS)):
            target = tbuf[it, 2 * k : 2 * k + 2, :]
            if k < SWEEPS - 1:
                target = target - couple_wait(SWEEPS - 1 + k)
            solve_send(SWEEPS + k, uw[k], target)
            raw = solve_wait(SWEEPS + k)
            if k > 0:
                lhs = spread(raw, 0, 8)
                out = dot_nt(lhs, factor(k - 1, k))
                if k < SWEEPS - 1:
                    out = out + cacc[k - 1]
                couple_send(SWEEPS - 1 + k - 1, fold(out, 2))
                for i in range(k - 1):
                    out = dot_nt(lhs, factor(i, k))
                    cacc[i] = out if k == SWEEPS - 1 else cacc[i] + out
            z = raw
            for j in range(ITERS):
                z = z - coef[it, j] * zs[j, 8 * k : 8 * k + 8, :]
            z = z / norm
            yz[8 * k : 8 * k + 8, :] = z
            lhs = spread(z, 0, 8)
            out = dot_nn(lhs, aw[k * 1024 : (k + 1) * 1024, :])
            wacc[...] = out if k == SWEEPS - 1 else wacc[...] + out
        zs[it] = yz[...]
        w = fold(wacc[...], 8) + jnp.where(own, DIAG_SHIFT * own_rows(yz), 0.0)
        u_ref[...] = exchange_w(it + 1, w) - alpha[...] * vs[it]
        return 0

    lax.fori_loop(0, ITERS, iterate, 0)
    send_dots(ITERS)
    finish_dots(ITERS)

    beta = coef[0, 3]
    zero = jnp.zeros((8, TILE), F32)
    hess = [[zero] * ITERS for _ in range(ITERS + 1)]
    for k in range(ITERS):
        for j in range(k + 1):
            hess[j][k] = coef[k + 1, j] + (coef[k + 1, 4] if j == k else 0.0)
        hess[k + 1][k] = coef[k + 1, 3]
    normal = [[sum(hess[i][a] * hess[i][d] for i in range(ITERS + 1)) for d in range(ITERS)] for a in range(ITERS)]
    rhs = [beta * hess[0][a] for a in range(ITERS)]
    low = [[None] * ITERS for _ in range(ITERS)]
    for a in range(ITERS):
        for d in range(a + 1):
            v = normal[a][d]
            for e in range(d):
                v = v - low[a][e] * low[d][e]
            low[a][d] = jnp.sqrt(v) if a == d else v / low[d][d]
    fwd = []
    for a in range(ITERS):
        v = rhs[a]
        for e in range(a):
            v = v - low[a][e] * fwd[e]
        fwd.append(v / low[a][a])
    wts = [None] * ITERS
    for a in reversed(range(ITERS)):
        v = fwd[a]
        for e in range(a + 1, ITERS):
            v = v - low[e][a] * wts[e]
        wts[a] = v / low[a][a]
    for k in range(SWEEPS):
        part = x0_ref[8 * k : 8 * k + 8, :]
        for a in range(ITERS):
            part = part + wts[a] * zs[a, 8 * k : 8 * k + 8, :]
        x_out[8 * k : 8 * k + 8, :] = part
    sub = lax.broadcasted_iota(jnp.int32, (8, TILE), 0)
    lane = lax.broadcasted_iota(jnp.int32, (8, TILE), 1)
    table = zero
    for j in range(ITERS + 1):
        for k in range(ITERS):
            if j <= k + 1:
                table = jnp.where((sub == j) & (lane == k), hess[j][k], table)
    h_out[...] = table

    def drain(it, _):
        for step in range(2 * SWEEPS):
            wait_bytes(ybuf.at[it, step, pl.ds(0, N_ROW - 1)], y_ssem)
        for step in range(2 * SWEEPS - 2):
            wait_bytes(cbuf.at[it, step, pl.ds(0, N_COL - 1)], c_ssem)
        return 0

    lax.fori_loop(0, ITERS, drain, 0)
    for index in range(ITERS + 1):
        wait_bytes(wbuf.at[index, pl.ds(0, N_COL - 1)], w_ssem)
        wait_bytes(dbuf.at[index, pl.ds(0, N_ROW - 1)], d_ssem)


def shards(tile_seeds, factors, lower_inverse, upper_inverse, right_side, first_guess):
    vmem = pl.BlockSpec(memory_space=pltpu.VMEM)
    hbm = pl.BlockSpec(memory_space=pl.ANY)
    dma = pltpu.SemaphoreType.DMA
    x, h = pl.pallas_call(
        kernel,
        out_shape=(jax.ShapeDtypeStruct((32, TILE), F32), jax.ShapeDtypeStruct((8, TILE), F32)),
        in_specs=[pl.BlockSpec(memory_space=pltpu.SMEM), hbm, hbm, hbm, vmem, vmem],
        out_specs=(vmem, vmem),
        scratch_shapes=[
            pltpu.VMEM((8, TILE, 32, TILE), BF16),
            pltpu.VMEM((2, 8192, TILE), BF16),
            pltpu.VMEM((4096, TILE), F32),
            pltpu.VMEM((1024, 4096), BF16),
            pltpu.VMEM((SWEEPS, 1024, 256), BF16),
            pltpu.VMEM((SWEEPS, 1024, 256), BF16),
            pltpu.VMEM((4096, 1024), BF16),
            pltpu.VMEM((TILE, TILE), jnp.int32),
            pltpu.VMEM((8, 8, TILE), F32),
            pltpu.VMEM((8, 1024), F32),
            pltpu.VMEM((SWEEPS, 8, 256), F32),
            pltpu.VMEM((32, TILE), F32),
            pltpu.VMEM((ITERS, 32, TILE), F32),
            pltpu.VMEM((ITERS, 8, TILE), F32),
            pltpu.VMEM((8, TILE), F32),
            pltpu.VMEM((ITERS + 1, 5, 8, TILE), F32),
            pltpu.VMEM((8, TILE), F32),
            pltpu.VMEM((ITERS, 2 * SWEEPS, N_ROW, 8, TILE), BF16),
            pltpu.VMEM((ITERS, 2 * SWEEPS - 2, N_COL, 2, TILE), F32),
            pltpu.VMEM((ITERS + 1, N_COL, 8, TILE), F32),
            pltpu.VMEM((ITERS + 1, N_ROW, 4, TILE), F32),
            pltpu.VMEM((ITERS, 8, TILE), F32),
            pltpu.VMEM((4, TILE), F32),
            dma((3,)), dma, dma, dma, dma, dma,
            dma((ITERS, 2 * SWEEPS)), dma((ITERS, 2 * SWEEPS - 2)), dma((ITERS + 1,)), dma((ITERS + 1,)), dma,
        ],
        compiler_params=pltpu.CompilerParams(collective_id=0, has_side_effects=True, vmem_limit_bytes=62 << 20),
        name="refine",
    )(
        tile_seeds.reshape(8, 32), factors, lower_inverse.reshape(8192, TILE), upper_inverse.reshape(8192, TILE),
        right_side, first_guess,
    )
    return x, h[: ITERS + 1, :ITERS]


def solution(mesh):
    in_specs = (
        P(None, "row", None, "col"),
        P(None, "row", None, "col"),
        P(None, None, "col", None, "row"),
        P(None, None, "col", None, "row"),
        P(None, "row"),
        P(None, "col"),
    )
    out_specs = (P(None, "col"), P())
    return jax.shard_map(shards, mesh=mesh, in_specs=in_specs, out_specs=out_specs, check_vma=False)
```

time: 946 us -> 282 us (0.30); the launches traced: 933 us -> 282 us
  blocking collectives: 320 us -> 0 us
  Pallas kernels: 0 us -> 279 us
  waiting for transfers between devices: 141 us -> 0 us
  matrix products: 118 us -> 0 us
  starting transfers between devices: 110 us -> 0 us
  other arithmetic: 109 us -> 0 us
  local copies, waits for them, and re-layouts: 96.5 us -> 2.57 us
  loops' own time: 22.1 us -> 0 us
  between operations: 17 us -> 0.64 us
    all_to_all x30 -> x0, blocking collectives: 320 us -> none  [from_everyone(): lax.all_to_all(jnp.broadcast_to(x[None], (size, *x.shape)), axis, 0, 0, t...]
    pallas_call x0 -> x1, Pallas kernels: none -> 279 us  [shards(): pl.pallas_call(kernel, out_shape=(jax.ShapeDtypeStruct((32, TILE), F32),...]
    all_to_all x23 -> x0, waiting for transfers between devices: 141 us -> none  [from_everyone(): lax.all_to_all(jnp.broadcast_to(x[None], (size, *x.shape)), axis, 0, 0, t...]
    dot_general x75 -> x0, matrix products: 118 us -> none  [the longest x32 86.8 us: one_row(): jnp.einsum('icj,cj->i', values, vector_col, precision=lax.Precision.HIGHEST)]
    all_to_all x23 -> x0, starting transfers between devices: 110 us -> none  [from_everyone(): lax.all_to_all(jnp.broadcast_to(x[None], (size, *x.shape)), axis, 0, 0, t...]
    add x97 -> x0, other arithmetic: 89.6 us -> none  [the longest x32 86.6 us: one_row(): values + jnp.where(row_ids[:, None, None] == col_ids[None, :, :], DIAG_SH...]
    add x32 -> x0, local copies, waits for them, and re-layouts: 22.3 us -> none  [scrambled(): hashed = tile_seed + flat_index * 1640531527]
    another operation x4 -> x0, loops' own time: 22.1 us -> none  [matrix_part(): lax.map(one_row, (seed_grid, jnp.arange(seed_grid.shape[0], dtype=jnp.int...]
  transfers between devices with their start and end apart: 23 -> 0, of which waited for: 23 -> 0; matrix products, arithmetic and copies ran while one was open for 4% -> 0% of each run, Pallas kernels for 0% -> 0%
where the time goes in v1:
time: 282 us
  Pallas kernels  279 us (99%)
    pallas_call x1, Pallas kernels, shards(): pl.pallas_call(kernel, out_shape=(jax.ShapeDtypeStruct((32, TILE), F32),...  279 us

profile of v1, /device:TPU:1, one launch (start us, length us, event | category | flops | bytes accessed | tf_op | source)
XLA Modules:
  0.0 282.1 jit_solution(5547101975677740689)
XLA Ops:
  0.6 278.9 %refine.1 = (f32[32,128]{1,0:T(8,128)}, f32[8,128]{1,0:T(8,128)}) custom-call(s32[8,32]{1,0:T(8,128)} %bitcast.5, bf16[8,128,32,128]{3,2,1,0:T(8,128)(2,1)} %f_hbm.1, bf16[8192,128]{1,0:T(8,128)(2,1)} %bitcast.3, bf16[8192,128]{1,0:T(8,128)(2,1)} %bitcast.4, f32[8,128]{1,0:T(8,128)} %b_ref.1, f32[32,128]{1,0:T(8,128)} %x0_ref.1), custom_call_target="tpu_custom_call" | custom-call | tf_op jit(solution)/shard_map/refine/pallas_call | solution.py:323
  279.5 1.2 slice.3
  280.8 1.3 copy.9

commit v2 on v1

--- a/solution.py
+++ b/solution.py
@@ -109,36 +109,42 @@
 
     lax.fori_loop(0, 32, make, 0)
 
-    f_copy.wait()
-
-    def lay_factor(q, _):
-        stage[...] = f_raw[q].astype(F32).reshape(TILE * 32, TILE)
-        for n in range(32):
-            part = stage[pl.ds(n, TILE, stride=32), :]
-            fw[pl.ds(q * TILE, TILE), n * TILE : (n + 1) * TILE] = part.astype(BF16)
-        return 0
-
-    lax.fori_loop(0, 8, lay_factor, 0)
-    l_copy.wait()
-    u_copy.wait()
-    for which, target in ((0, lw), (1, uw)):
-
-        def lay_inverse(k, _):
-            stage[pl.ds(0, 2048), :] = i_raw[which, pl.ds(k * 2048, 2048), :].astype(F32)
-            for m in range(2):
-                target[k, :, m * TILE : (m + 1) * TILE] = stage[pl.ds(m, 1024, stride=2), :].astype(BF16)
+    def lay_out():
+        l_copy.wait()
+        u_copy.wait()
+        for which, target in ((0, lw), (1, uw)):
+
+            def lay_inverse(k, _):
+                stage[pl.ds(0, 2048), :] = i_raw[which, pl.ds(k * 2048, 2048), :].astype(F32)
+                for m in range(2):
+                    target[k, :, m * TILE : (m + 1) * TILE] = stage[pl.ds(m, 1024, stride=2), :].astype(BF16)
+                return 0
+
+            lax.fori_loop(0, SWEEPS, lay_inverse, 0)
+        f_copy.wait()
+
+        def lay_factor(q, _):
+            for g in range(4):
+                rows = f_raw[q, :, 8 * g : 8 * g + 8, :].astype(F32)
+                stage[g * 1024 : (g + 1) * 1024, :] = rows.reshape(1024, TILE)
+                for n in range(8):
+                    part = stage[pl.ds(g * 1024 + n, TILE, stride=8), :]
+                    at = (8 * g + n) * TILE
+                    fw[pl.ds(q * TILE, TILE), at : at + TILE] = part.astype(BF16)
             return 0
 
-        lax.fori_loop(0, SWEEPS, lay_inverse, 0)
+        lax.fori_loop(0, 8, lay_factor, 0)
 
     pl.semaphore_wait(barrier, len(rows_of) + len(cols_of))
 
     def own_rows(ref):
         return ref[pl.ds(quarter, 8, stride=4), :]
 
-    def exchange_w(index, partial):
+    def exchange_w(index, partial, between=None):
         wbuf[index, c] = partial
         send(wbuf.at[index, c], cols_of, w_ssem, w_rsem.at[index])
+        if between is not None:
+            between()
         wait_bytes(wbuf.at[index, pl.ds(0, N_COL - 1)], w_rsem.at[index])
         return jnp.sum(wbuf[index], axis=0)
 
@@ -163,7 +169,7 @@
 
     w0 = jnp.concatenate([jnp.sum(racc[tr], axis=0, keepdims=True) for tr in range(8)], axis=0)
     w0 = w0 + jnp.where(own, DIAG_SHIFT * own_rows(x0_ref), 0.0)
-    u_ref[...] = b_ref[...] - exchange_w(0, w0)
+    u_ref[...] = b_ref[...] - exchange_w(0, w0, lay_out)
     vs[...] = jnp.zeros_like(vs)
     zs[...] = jnp.zeros_like(zs)
     alpha[...] = jnp.full((8, TILE), DIAG_SHIFT, F32)

time: 282 us -> 269 us (0.954)
  Pallas kernels: 279 us -> 266 us
    pallas_call x1, Pallas kernels: 279 us -> 266 us  [shards(): pl.pallas_call(kernel, out_shape=(jax.ShapeDtypeStruct((32, TILE), F32),...]
where the time goes in v2:
time: 269 us
  Pallas kernels  266 us (99%)
    pallas_call x1, Pallas kernels, shards(): pl.pallas_call(kernel, out_shape=(jax.ShapeDtypeStruct((32, TILE), F32),...  266 us

profile of v2, /device:TPU:1, one launch (start us, length us, event | category | flops | bytes accessed | tf_op | source)
XLA Modules:
  0.0 268.9 jit_solution(607250541571216810)
XLA Ops:
  0.6 265.7 %refine.1 = (f32[32,128]{1,0:T(8,128)}, f32[8,128]{1,0:T(8,128)}) custom-call(s32[8,32]{1,0:T(8,128)} %bitcast.5, bf16[8,128,32,128]{3,2,1,0:T(8,128)(2,1)} %f_hbm.1, bf16[8192,128]{1,0:T(8,128)(2,1)} %bitcast.3, bf16[8192,128]{1,0:T(8,128)(2,1)} %bitcast.4, f32[8,128]{1,0:T(8,128)} %b_ref.1, f32[32,128]{1,0:T(8,128)} %x0_ref.1), custom_call_target="tpu_custom_call" | custom-call | tf_op jit(solution)/shard_map/refine/pallas_call | solution.py:329
  266.3 1.2 slice.3
  267.6 1.3 copy.9
